TPU v7x, 256 devices: a 2x2x32 block of a 4x8x32 slice. The times are simulated.
256 devices in a mesh: grp: 4 (over y, x), panel: 64 (over z, core).
Axes of the slice: x: 2, y: 2, z: 32, core: 2. Of those that a mesh axis runs over, the one named last changes fastest.
The devices are a block of a 4x8x32 slice.
Arguments:
- density: bfloat16 [8192, 16, 128], P(('grp', 'panel')), parts along dimension 0, may hold values from -6 to 6
- near_blocks: bfloat16 [8192, 8, 128, 128], P(('grp', 'panel')), parts along dimension 0, may hold values from -0.1875 to 0.1875
- neighbours: int32 [8192, 8], P(('grp', 'panel')), parts along dimension 0, may hold values from 0 to 2047, as said below
- counts: int32 [8192], P(('grp', 'panel')), parts along dimension 0, may hold values from 1 to 8, as said below
- coarse_map: int32 [8192], P(('grp', 'panel')), parts along dimension 0, may hold values from 0 to 127, as said below
- restrict: bfloat16 [8192, 128, 128], P(('grp', 'panel')), parts along dimension 0, may hold values from -0.125 to 0.125
- evaluate: bfloat16 [8192, 128, 128], P(('grp', 'panel')), parts along dimension 0, may hold values from -0.5 to 0.5
- coupling: float32 [512, 128], P(('grp', 'panel')), parts along dimension 0, as said below
Outputs:
- potential: bfloat16 [8192, 16, 128], P(('grp', 'panel')), parts along dimension 0
There are 4 independent parts, one for each index of `grp`. A program takes and returns all parts, laid end to end along the dimension named above; each array names one. Nothing has to cross between parts.
Inputs may be any that keep to these rules, and one draw needn't show every extreme that they name: `neighbours`: slot 0 of block b is b itself; every entry lies within 16 blocks of b; in every draw some entry lies exactly 16 blocks below its block and some exactly 16 above. `counts`: every device holds blocks with all 8 slots live. `coarse_map`: block b's coarse cluster is one of the 2 clusters from (b // 32) * 2 on. `coupling`: the matrix is symmetric.
All inputs are finite; a program needn't handle non-finite values.
Results may differ from a plain program's by a relative error of at most 0.0042.
Values may be sent and summed in bfloat16 or wider, within the bound.
A program may use at most 64 MiB of HBM per device.

v0:
```python
import jax
import jax.numpy as jnp
from jax import lax
from jax.sharding import Mesh
from jax.sharding import PartitionSpec as P

PANEL = ("panel_0", "panel_1")
GRP_PANEL = ("grp", "panel_0", "panel_1")


def extended_2(block, sides, width):
    for axis, dim in sides:
        count = lax.axis_size(axis)
        forward = [(i, i + 1) for i in range(count - 1)]
        backward = [(target, source) for source, target in forward]
        low = lax.ppermute(
            lax.slice_in_dim(block, block.shape[dim] - width, None, axis=dim), axis, forward
        )
        high = lax.ppermute(lax.slice_in_dim(block, 0, width, axis=dim), axis, backward)
        block = jnp.concatenate([low, block, high], axis=dim)
    return block


def joined_along(pieces, dim):
    pieces = jnp.moveaxis(pieces, 0, dim)
    lengths = pieces.shape
    return pieces.reshape(*lengths[:dim], lengths[dim] * lengths[dim + 1], *lengths[dim + 2 :])


def gather_in_order(array, axes, order):
    pieces = array[None]
    for k in order:
        pieces = lax.all_gather(pieces, axes[k], axis=0, tiled=True)
    held = [lax.axis_size(axes[k]) for k in reversed(order)]
    pieces = pieces.reshape(*held, *array.shape)
    turned = sorted(range(len(order)), key=lambda place: order[len(order) - 1 - place])
    return pieces.transpose(*turned, *range(len(order), pieces.ndim)).reshape(-1, *array.shape)


def gather_axes(array, axes, order, dim):
    return joined_along(gather_in_order(array, axes, order), dim)


def shards(density, near_blocks, neighbours, counts, coarse_map, restrict, evaluate, coupling):
    blk_count, columns, panels = density.shape
    reach_blocks = blk_count // 2
    anchor = lax.axis_index(PANEL) * blk_count
    extended = extended_2(density, ((PANEL, 0),), reach_blocks)
    local_ids = neighbours - (anchor - reach_blocks)
    picked = jnp.take(extended, local_ids, axis=0)
    slot_ids = jnp.arange(neighbours.shape[1])
    live_slots = slot_ids[None, :] < counts[:, None]
    picked = jnp.where(live_slots[:, :, None, None], picked, jnp.zeros((), jnp.bfloat16))
    near_part = jnp.einsum(
        "bjpq,bjrq->brp", near_blocks, picked, preferred_element_type=jnp.float32
    )
    coarse_dev = coupling.shape[0]
    expand_terms = restrict.shape[1]
    block_terms = jnp.einsum("bkp,brp->brk", restrict, density, preferred_element_type=jnp.float32)
    block_terms = block_terms.reshape(blk_count, columns * expand_terms)
    own_ids = coarse_map - lax.axis_index(PANEL) * coarse_dev
    onehot = (own_ids[None, :] == jnp.arange(coarse_dev)[:, None]).astype(jnp.float32)
    moments = jnp.dot(onehot, block_terms, precision=lax.Precision.HIGHEST)
    all_moments = gather_axes(moments, PANEL, (0, 1), 0)
    local_full = jnp.dot(coupling, all_moments, precision=lax.Precision.HIGHEST)
    local_exp = local_full.astype(jnp.bfloat16)
    spread = jnp.dot(onehot.T.astype(jnp.bfloat16), local_exp, preferred_element_type=jnp.float32)
    spread = spread.astype(jnp.bfloat16).reshape(blk_count, columns, expand_terms)
    far_part = jnp.einsum("bkp,brk->brp", evaluate, spread, preferred_element_type=jnp.float32)
    return (near_part + far_part).astype(jnp.bfloat16)


def solution(mesh):
    torus = Mesh(mesh.devices.reshape(mesh.shape["grp"], 32, 2), ("grp", "panel_0", "panel_1"))
    placed = (
        P(GRP_PANEL, None, None),
        P(GRP_PANEL, None, None, None),
        P(GRP_PANEL, None),
        P(GRP_PANEL),
        P(GRP_PANEL),
        P(GRP_PANEL, None, None),
        P(GRP_PANEL, None, None),
        P(GRP_PANEL, None),
    )
    return jax.shard_map(
        shards, mesh=torus, in_specs=placed, out_specs=P(GRP_PANEL, None, None), check_vma=False
    )
```

profile of v0, /device:TPU:37, one launch (start us, length us, event | category | flops | bytes accessed | tf_op | source)
XLA Modules:
  0.0 128.4 jit_solution(989126953056692734)
XLA Ops:
  6.5 0.0 copy-start
  6.6 0.0 all-gather.4.cloned.1.call-start
  6.6 1.0 fusion.16
  7.5 5.1 %collective-permute-start = (bf16[16,16,128]{2,1,0:T(8,128)(2,1)S(1)}, bf16[16,16,128]{2,1,0:T(8,128)(2,1)S(1)}, u32[]{:S(2)}, u32[]{:S(2)}) collective-permute-start(bf16[16,16,128]{2,1,0:T(8,128)(2,1)S(1)} %get-tuple-element.7), channel_id=1, source_target_pairs={{0,1},{1,2},{2,3},{3,4},{4,5},{5,6},{6,7},{7,8},{8,9},{9,10},{10,1... | collective-permute-start | bytes 196616 | tf_op jit(solution)/shard_map/ppermute | solution.py:16
  12.6 18.6 %collective-permute-start.1 = (bf16[16,16,128]{2,1,0:T(8,128)(2,1)S(1)}, bf16[16,16,128]{2,1,0:T(8,128)(2,1)S(1)}, u32[]{:S(2)}, u32[]{:S(2)}) collective-permute-start(bf16[16,16,128]{2,1,0:T(8,128)(2,1)S(1)} %get-tuple-element.8), channel_id=1, source_target_pairs={{1,0},{2,1},{3,2},{4,3},{5,4},{6,5},{7,6},{8,7},{9,8},{10,9},{11,1... | collective-permute-start | bytes 196616 | tf_op jit(solution)/shard_map/ppermute | solution.py:19
  31.2 0.0 copy-done
  31.2 1.5 %fusion.17 = f32[32,16,128]{2,1,0:T(8,128)S(1)} fusion(bf16[32,16,128]{2,1,0:T(8,128)(2,1)} %param.8, bf16[32,128,128]{2,1,0:T(8,128)(2,1)S(1)} %copy-done), kind=kOutput, calls=%fused_computation.32 | convolution fusion | flops 16777216 | bytes 1441792 | tf_op jit(solution)/shard_map/bkp,brp->brk/dot_general | solution.py:59
  32.8 0.7 broadcast_subtract_fusion
  33.4 0.3 convolution_bitcast_fusion
  33.7 49.7 %all-gather.1 = f32[32,2,2048]{2,1,0:T(2,128)} all-gather(f32[1,2,2048]{2,1,0:T(2,128)S(1)} %convolution_bitcast_fusion), channel_id=2, replica_groups=mesh['grp'=4,'panel_0'=32,'panel_1'=2] {'panel_0'}, dimensions={0}, use_global_device_ids=true | all-gather | bytes 540672 | tf_op jit(solution)/shard_map/all_gather | solution.py:33
  83.4 0.1 all-gather.4.cloned.1.call-update
  83.5 0.7 compare_and_fusion
  84.2 0.1 copy.14
  84.2 0.1 reshape.41
  84.3 0.1 copy.13
  84.4 0.7 iota_compare_fusion.1
  85.1 0.0 copy-start.1
  85.2 0.0 collective-permute-done
  85.2 0.0 collective-permute-done.1
  85.2 0.9 pad_maximum_fusion
  86.1 0.8 gather_fusion
  87.0 4.7 %convolution_bitcast_fusion.1 = f32[32,16,128]{2,1,0:T(8,128)S(1)} fusion(bf16[32,8,128,128]{3,2,1,0:T(8,128)(2,1)} %param.9, bf16[32,8,16,128]{3,2,1,0:T(8,128)(2,1)S(1)} %bitcast.27, pred[32,8]{1,0:T(8,128)(4,1)S(1)} %copy.13, pred[32,8]{1,0:T(8,128)(4,1)S(1)} %iota_compare_fusion.1), kind=kOutput, calls=%fused_computation.5 | convolution fusion | flops 135266304 | bytes 9699840 | tf_op jit(solution)/shard_map/bjpq,bjrq->brp/dot_general | solution.py:54
  91.7 24.6 %all-gather.4.cloned.1.call-done = f32[64,2,2048]{2,1,0:T(2,128)} async-done(((f32[32,2,2048]{2,1,0:T(2,128)}), f32[64,2,2048]{2,1,0:T(2,128)}) %all-gather.4.cloned.1.call-update) | async-done | bytes 1048592 | tf_op jit(solution)/shard_map/all_gather | solution.py:33
  116.3 1.3 %copy.24 = f32[2,32,2,2048]{3,2,0,1:T(2,128)S(1)} copy(f32[2,32,2,2048]{3,2,1,0:T(2,128)} %bitcast.26) | data formatting | bytes 2097152 | tf_op jit(solution)/shard_map/reshape | solution.py:35
  117.6 0.7 reshape_reshape.3
  118.4 0.0 copy-done.1
  118.4 0.7 convolution_convert_fusion.1
  119.0 0.2 fusion.1
  119.3 2.3 %fusion = bf16[32,16,128]{2,1,0:T(8,128)(2,1)} fusion(f32[32,16,128]{2,1,0:T(8,128)S(1)} %convolution_bitcast_fusion.1, bf16[32,16,128]{2,1,0:T(8,128)(2,1)S(1)} %bitcast.29, bf16[32,128,128]{2,1,0:T(8,128)(2,1)} %param.14), kind=kOutput, calls=%fused_computation.6 | convolution fusion | flops 16908288 | bytes 1572864 | tf_op jit(solution)/shard_map/bkp,brk->brp/dot_general | solution.py:69
  (2 shorter events, 0.0 us)
Async XLA Ops:
  6.5 24.7 %copy-start = (bf16[32,128,128]{2,1,0:T(8,128)(2,1)S(1)}, bf16[32,128,128]{2,1,0:T(8,128)(2,1)}, u32[]{:S(2)}) copy-start(bf16[32,128,128]{2,1,0:T(8,128)(2,1)} %param.13) | copy-start | bytes 3145732
  6.6 109.8 %all-gather.4.cloned.1.call-start = ((), (), s32[]{:S(2)}) async-start(), calls=%async_computation | async-start | bytes 1572864 | tf_op jit(solution)/shard_map/all_gather | solution.py:33
  7.5 77.6 %collective-permute-start = (bf16[16,16,128]{2,1,0:T(8,128)(2,1)S(1)}, bf16[16,16,128]{2,1,0:T(8,128)(2,1)S(1)}, u32[]{:S(2)}, u32[]{:S(2)}) collective-permute-start(bf16[16,16,128]{2,1,0:T(8,128)(2,1)S(1)} %get-tuple-element.7), channel_id=1, source_target_pairs={{0,1},{1,2},{2,3},{3,4},{4,5},{5,6},{6,7},{7,8},{8,9},{9,10},{10,1... | collective-permute-start | bytes 196616 | tf_op jit(solution)/shard_map/ppermute | solution.py:16
  12.6 72.5 %collective-permute-start.1 = (bf16[16,16,128]{2,1,0:T(8,128)(2,1)S(1)}, bf16[16,16,128]{2,1,0:T(8,128)(2,1)S(1)}, u32[]{:S(2)}, u32[]{:S(2)}) collective-permute-start(bf16[16,16,128]{2,1,0:T(8,128)(2,1)S(1)} %get-tuple-element.8), channel_id=1, source_target_pairs={{1,0},{2,1},{3,2},{4,3},{5,4},{6,5},{7,6},{8,7},{9,8},{10,9},{11,1... | collective-permute-start | bytes 196616 | tf_op jit(solution)/shard_map/ppermute | solution.py:19
  85.1 33.2 %copy-start.1 = (f32[2,128]{1,0:T(2,128)S(1)}, f32[2,128]{1,0:T(2,128)}, u32[]{:S(2)}) copy-start(f32[2,128]{1,0:T(2,128)} %param.15) | copy-start | bytes 3076
Sparse Core Ops, SparseCore 0:
  83.6 32.6 all-gather.3
where the time goes:
time: 129 us; the launch traced here: 128 us
  blocking collectives  49.7 us (39%)
  waiting for transfers between devices  24.7 us (19%)
  starting transfers between devices  23.7 us (18%)
  between operations  13.5 us (10%)
  matrix products  9.67 us (7%)
  local copies, waits for them, and re-layouts  4.13 us (3%)
  other arithmetic  3.06 us (2%)
    all_gather x1, blocking collectives, gather_in_order(): pieces = lax.all_gather(pieces, axes[k], axis=0, tiled=True)  49.7 us
    all_gather x1, waiting for transfers between devices, gather_in_order(): pieces = lax.all_gather(pieces, axes[k], axis=0, tiled=True)  24.6 us
    ppermute x1, starting transfers between devices, extended_2(): lax.ppermute(lax.slice_in_dim(block, 0, width, axis=dim), axis, backward)  18.6 us
    ppermute x1, starting transfers between devices, extended_2(): lax.ppermute(lax.slice_in_dim(block, block.shape[dim] - width, None, axis...  5.09 us
    dot_general x1, matrix products, shards(): jnp.einsum('bjpq,bjrq->brp', near_blocks, picked, preferred_element_type=...  4.7 us
  transfers between devices with their start and end apart: 3, of which 1 were waited for; matrix products, arithmetic and copies ran while one was open for 8% of the time, Pallas kernels for 0%

commit v1 on v0

--- a/solution.py
+++ b/solution.py
@@ -6,6 +6,15 @@
 
 PANEL = ("panel_0", "panel_1")
 GRP_PANEL = ("grp", "panel_0", "panel_1")
+track_case = lambda unit, named_axis: jnp.concatenate(
+    jax.lax.all_to_all(
+        jnp.stack([unit for _ in range(jax.lax.psum(1, named_axis))]),
+        axis_name=named_axis,
+        split_axis=0,
+        concat_axis=0,
+    ),
+    0,
+)
 
 
 def extended_2(block, sides, width):
@@ -30,7 +39,7 @@
 def gather_in_order(array, axes, order):
     pieces = array[None]
     for k in order:
-        pieces = lax.all_gather(pieces, axes[k], axis=0, tiled=True)
+        pieces = track_case(pieces, axes[k])
     held = [lax.axis_size(axes[k]) for k in reversed(order)]
     pieces = pieces.reshape(*held, *array.shape)
     turned = sorted(range(len(order)), key=lambda place: order[len(order) - 1 - place])

time: 129 us -> 112 us (0.87)
  blocking collectives: 49.7 us -> 6.77 us
  waiting for transfers between devices: 24.7 us -> 48 us
  starting transfers between devices: 23.7 us -> 38.9 us
  between operations: 13.5 us -> 0.11 us
    all_gather x1 -> x0, blocking collectives: 49.7 us -> none  [gather_in_order(): pieces = lax.all_gather(pieces, axes[k], axis=0, tiled=True)]
    all_to_all x0 -> x1, starting transfers between devices: none -> 33.2 us  [jax.lax.all_to_all(jnp.stack([unit for _ in range(jax.lax.psum(1, named_a...]
    all_gather x1 -> x0, waiting for transfers between devices: 24.6 us -> none  [gather_in_order(): pieces = lax.all_gather(pieces, axes[k], axis=0, tiled=True)]
    ppermute x1, waiting for transfers between devices: 0.01 us -> 22.3 us  [extended_2(): lax.ppermute(lax.slice_in_dim(block, block.shape[dim] - width, None, axis...]
    ppermute x1, starting transfers between devices: 18.6 us -> 1.95 us  [extended_2(): lax.ppermute(lax.slice_in_dim(block, 0, width, axis=dim), axis, backward)]
    ppermute x1, waiting for transfers between devices: 0.01 us -> 13.4 us  [extended_2(): lax.ppermute(lax.slice_in_dim(block, 0, width, axis=dim), axis, backward)]
    all_to_all x0 -> x1, waiting for transfers between devices: none -> 12.3 us  [jax.lax.all_to_all(jnp.stack([unit for _ in range(jax.lax.psum(1, named_a...]
    all_to_all x0 -> x1, blocking collectives: none -> 6.77 us  [jax.lax.all_to_all(jnp.stack([unit for _ in range(jax.lax.psum(1, named_a...]
  transfers between devices with their start and end apart: 3 -> 3, of which waited for: 1 -> 3; matrix products, arithmetic and copies ran while one was open for 8% -> 8% of each run, Pallas kernels for 0% -> 0%
where the time goes in v1:
time: 112 us; the launch traced here: 111 us
  waiting for transfers between devices  48 us (43%)
  starting transfers between devices  38.9 us (35%)
  matrix products  9.68 us (9%)
  blocking collectives  6.77 us (6%)
  local copies, waits for them, and re-layouts  4.35 us (4%)
  other arithmetic  3.6 us (3%)
    all_to_all x1, starting transfers between devices, jax.lax.all_to_all(jnp.stack([unit for _ in range(jax.lax.psum(1, named_a...  33.2 us
    ppermute x1, waiting for transfers between devices, extended_2(): lax.ppermute(lax.slice_in_dim(block, block.shape[dim] - width, None, axis...  22.3 us
    ppermute x1, waiting for transfers between devices, extended_2(): lax.ppermute(lax.slice_in_dim(block, 0, width, axis=dim), axis, backward)  13.4 us
    all_to_all x1, waiting for transfers between devices, jax.lax.all_to_all(jnp.stack([unit for _ in range(jax.lax.psum(1, named_a...  12.3 us
    all_to_all x1, blocking collectives, jax.lax.all_to_all(jnp.stack([unit for _ in range(jax.lax.psum(1, named_a...  6.77 us
    dot_general x1, matrix products, shards(): jnp.einsum('bjpq,bjrq->brp', near_blocks, picked, preferred_element_type=...  4.7 us
    ppermute x1, starting transfers between devices, extended_2(): lax.ppermute(lax.slice_in_dim(block, block.shape[dim] - width, None, axis...  3.76 us
    dot_general x1, matrix products, shards(): jnp.einsum('bkp,brk->brp', evaluate, spread, preferred_element_type=jnp.f...  2.28 us
  transfers between devices with their start and end apart: 3, of which 3 were waited for; matrix products, arithmetic and copies ran while one was open for 8% of the time, Pallas kernels for 0%

profile of v1, /device:TPU:37, one launch (start us, length us, event | category | flops | bytes accessed | tf_op | source)
XLA Modules:
  0.0 111.4 jit_solution(16117069117862113670)
XLA Ops:
  0.0 0.0 copy-start
  0.0 0.7 broadcast_subtract_fusion
  0.8 0.5 copy-done
  1.2 1.5 %fusion.18 = f32[32,16,128]{2,1,0:T(8,128)S(1)} fusion(bf16[32,16,128]{2,1,0:T(8,128)(2,1)} %param.8, bf16[32,128,128]{2,1,0:T(8,128)(2,1)S(1)} %copy-done), kind=kOutput, calls=%fused_computation.32 | convolution fusion | flops 16777216 | bytes 1441792 | tf_op jit(solution)/shard_map/bkp,brp->brk/dot_general | solution.py:68
  2.8 0.3 fusion.8
  3.1 1.0 stack.6
  4.1 33.2 %all-to-all-start = ((f32[32,1,2,2048]{3,2,1,0:T(2,128)}), f32[32,1,2,2048]{3,2,1,0:T(2,128)S(1)}, u32[]{:S(2)}, u32[]{:S(2)}) async-start(f32[32,1,2,2048]{3,2,1,0:T(2,128)} %stack.6), calls=%async_computation | async-start | bytes 1048576 | tf_op jit(solution)/shard_map/all_to_all | solution.py:10
  37.3 0.9 fusion.17
  38.2 3.8 %collective-permute-start = (bf16[16,16,128]{2,1,0:T(8,128)(2,1)S(1)}, bf16[16,16,128]{2,1,0:T(8,128)(2,1)S(1)}, u32[]{:S(2)}, u32[]{:S(2)}) collective-permute-start(bf16[16,16,128]{2,1,0:T(8,128)(2,1)S(1)} %get-tuple-element.7), channel_id=1, source_target_pairs={{0,1},{1,2},{2,3},{3,4},{4,5},{5,6},{6,7},{7,8},{8,9},{9,10},{10,1... | collective-permute-start | bytes 196616 | tf_op jit(solution)/shard_map/ppermute | solution.py:25
  42.0 2.0 %collective-permute-start.1 = (bf16[16,16,128]{2,1,0:T(8,128)(2,1)S(1)}, bf16[16,16,128]{2,1,0:T(8,128)(2,1)S(1)}, u32[]{:S(2)}, u32[]{:S(2)}) collective-permute-start(bf16[16,16,128]{2,1,0:T(8,128)(2,1)S(1)} %get-tuple-element.8), channel_id=1, source_target_pairs={{1,0},{2,1},{3,2},{4,3},{5,4},{6,5},{7,6},{8,7},{9,8},{10,9},{11,1... | collective-permute-start | bytes 196616 | tf_op jit(solution)/shard_map/ppermute | solution.py:28
  43.9 0.7 compare_and_fusion
  44.6 0.1 copy.13
  44.7 0.1 reshape.39
  44.8 0.1 copy.12
  44.9 0.7 iota_compare_fusion.1
  45.6 22.3 %collective-permute-done = bf16[16,16,128]{2,1,0:T(8,128)(2,1)S(1)} collective-permute-done((bf16[16,16,128]{2,1,0:T(8,128)(2,1)S(1)}, bf16[16,16,128]{2,1,0:T(8,128)(2,1)S(1)}, u32[]{:S(2)}, u32[]{:S(2)}) %collective-permute-start) | collective-permute-done | bytes 65568 | tf_op jit(solution)/shard_map/ppermute | solution.py:25
  67.9 13.4 %collective-permute-done.1 = bf16[16,16,128]{2,1,0:T(8,128)(2,1)S(1)} collective-permute-done((bf16[16,16,128]{2,1,0:T(8,128)(2,1)S(1)}, bf16[16,16,128]{2,1,0:T(8,128)(2,1)S(1)}, u32[]{:S(2)}, u32[]{:S(2)}) %collective-permute-start.1) | collective-permute-done | bytes 65568 | tf_op jit(solution)/shard_map/ppermute | solution.py:28
  81.3 0.9 pad_maximum_fusion.1
  82.2 0.9 gather_fusion
  83.1 0.0 copy-start.1
  83.1 4.7 %convolution_bitcast_fusion = f32[32,16,128]{2,1,0:T(8,128)S(1)} fusion(bf16[32,8,128,128]{3,2,1,0:T(8,128)(2,1)} %param.9, bf16[32,8,16,128]{3,2,1,0:T(8,128)(2,1)S(1)} %bitcast.23, pred[32,8]{1,0:T(8,128)(4,1)S(1)} %copy.12, pred[32,8]{1,0:T(8,128)(4,1)S(1)} %iota_compare_fusion.1), kind=kOutput, calls=%fused_computation.4 | convolution fusion | flops 135266304 | bytes 9699840 | tf_op jit(solution)/shard_map/bjpq,bjrq->brp/dot_general | solution.py:63
  87.8 12.3 %all-to-all-done = f32[32,1,2,2048]{3,2,1,0:T(2,128)S(1)} async-done(((f32[32,1,2,2048]{3,2,1,0:T(2,128)}), f32[32,1,2,2048]{3,2,1,0:T(2,128)S(1)}, u32[]{:S(2)}, u32[]{:S(2)}) %all-to-all-start) | async-done | bytes 524320 | tf_op jit(solution)/shard_map/all_to_all | solution.py:10
  100.1 0.5 pad_maximum_fusion
  100.6 6.8 %all_to_all.10 = f32[2,32,2,2048]{3,2,1,0:T(2,128)S(1)} all-to-all(f32[2,32,2,2048]{3,2,1,0:T(2,128)S(1)} %pad_maximum_fusion), channel_id=1, replica_groups=mesh['grp'=4,'panel_0'=32,'panel_1'=2] {'panel_1'}, dimensions={0} | all-to-all | bytes 2097152 | tf_op jit(solution)/shard_map/all_to_all | solution.py:10
  107.4 0.1 copy.14
  107.5 0.7 reshape_reshape.3
  108.2 0.0 copy-done.1
  108.2 0.7 convolution_convert_fusion.1
  108.8 0.2 fusion.1
  109.1 2.3 %fusion = bf16[32,16,128]{2,1,0:T(8,128)(2,1)} fusion(f32[32,16,128]{2,1,0:T(8,128)S(1)} %convolution_bitcast_fusion, bf16[32,16,128]{2,1,0:T(8,128)(2,1)S(1)} %bitcast.25, bf16[32,128,128]{2,1,0:T(8,128)(2,1)} %param.14), kind=kOutput, calls=%fused_computation.5 | convolution fusion | flops 16908288 | bytes 1572864 | tf_op jit(solution)/shard_map/bkp,brk->brp/dot_general | solution.py:78
  (2 shorter events, 0.0 us)
Async XLA Ops:
  0.0 1.2 %copy-start = (bf16[32,128,128]{2,1,0:T(8,128)(2,1)S(1)}, bf16[32,128,128]{2,1,0:T(8,128)(2,1)}, u32[]{:S(2)}) copy-start(bf16[32,128,128]{2,1,0:T(8,128)(2,1)} %param.13) | copy-start | bytes 3145732
  4.1 96.0 %all-to-all-start = ((f32[32,1,2,2048]{3,2,1,0:T(2,128)}), f32[32,1,2,2048]{3,2,1,0:T(2,128)S(1)}, u32[]{:S(2)}, u32[]{:S(2)}) async-start(f32[32,1,2,2048]{3,2,1,0:T(2,128)} %stack.6), calls=%async_computation | async-start | bytes 1048576 | tf_op jit(solution)/shard_map/all_to_all | solution.py:10
  38.2 29.7 %collective-permute-start = (bf16[16,16,128]{2,1,0:T(8,128)(2,1)S(1)}, bf16[16,16,128]{2,1,0:T(8,128)(2,1)S(1)}, u32[]{:S(2)}, u32[]{:S(2)}) collective-permute-start(bf16[16,16,128]{2,1,0:T(8,128)(2,1)S(1)} %get-tuple-element.7), channel_id=1, source_target_pairs={{0,1},{1,2},{2,3},{3,4},{4,5},{5,6},{6,7},{7,8},{8,9},{9,10},{10,1... | collective-permute-start | bytes 196616 | tf_op jit(solution)/shard_map/ppermute | solution.py:25
  42.0 39.3 %collective-permute-start.1 = (bf16[16,16,128]{2,1,0:T(8,128)(2,1)S(1)}, bf16[16,16,128]{2,1,0:T(8,128)(2,1)S(1)}, u32[]{:S(2)}, u32[]{:S(2)}) collective-permute-start(bf16[16,16,128]{2,1,0:T(8,128)(2,1)S(1)} %get-tuple-element.8), channel_id=1, source_target_pairs={{1,0},{2,1},{3,2},{4,3},{5,4},{6,5},{7,6},{8,7},{9,8},{10,9},{11,1... | collective-permute-start | bytes 196616 | tf_op jit(solution)/shard_map/ppermute | solution.py:28
  83.1 25.1 %copy-start.1 = (f32[2,128]{1,0:T(2,128)S(1)}, f32[2,128]{1,0:T(2,128)}, u32[]{:S(2)}) copy-start(f32[2,128]{1,0:T(2,128)} %param.15) | copy-start | bytes 3076
